TPU v7x, 32 devices: a whole 2x2x4 slice. The times are simulated.
32 devices in a mesh: gx: 2 (over x), gy: 4 (over z), gz: 4 (over y, core).
Axes of the slice: x: 2, y: 2, z: 4, core: 2. Of those that a mesh axis runs over, the one named last changes fastest.
Arguments:
- tokens: bfloat16 [512, 49, 512], P(('gx', 'gy', 'gz')), may hold values from -6 to 6
- cotangent: bfloat16 [512, 49, 512], P(('gx', 'gy', 'gz')), may hold values from -6 to 6
- regions: int32 [512, 49], P(('gx', 'gy', 'gz')), may hold values from 0 to 3
- rel_index: int32 [49, 49], replicated, may hold values from 0 to 168
- w_qkv: bfloat16 [512, 1536], replicated, may hold values from -0.25 to 0.25
- w_proj: bfloat16 [512, 512], replicated, may hold values from -0.25 to 0.25
- bias_table: float32 [169, 16], replicated, may hold values from -4 to 4
- mom_qkv: float32 [786432], P(('gx', 'gy', 'gz')), may hold values from -0.06 to 0.06
- mom_proj: float32 [262144], P(('gx', 'gy', 'gz')), may hold values from -0.06 to 0.06
- mom_table: float32 [169, 16], replicated, may hold values from -0.06 to 0.06
Outputs:
- new_mom_qkv: float32 [786432], P(('gx', 'gy', 'gz'))
- new_mom_proj: float32 [262144], P(('gx', 'gy', 'gz'))
- new_mom_table: float32 [169, 16], replicated
All inputs are finite; a program needn't handle non-finite values.
Results may differ from a plain program's by a relative error of at most 0.015.
Values sent between devices are 32-bit elements; how exact they have to be, the bound alone decides.
A program may use at most 128 MiB of HBM per device.

v0:
```python
import functools
import math

import jax
import jax.numpy as jnp
from jax import lax
from jax.experimental import pallas as pl
from jax.experimental.pallas import tpu as pltpu
from jax.sharding import PartitionSpec as P

AXES = ("gx", "gy", "gz")
MESH = pl.DeviceIdType.MESH
F32, BF16 = jnp.float32, jnp.bfloat16
PAD = 64
GROUP = 4
LOG2E = math.log2(math.e)
STEPS = 5
NT = (((1,), (1,)), ((), ()))
TN = (((0,), (0,)), ((), ()))


def dot(a, b, dims=(((1,), (0,)), ((), ()))):
    return lax.dot_general(a, b, dims, preferred_element_type=F32)


def spread(value, lanes, width):
    return jnp.concatenate(
        [jnp.where(lanes // width == h, value, jnp.zeros_like(value)) for h in range(GROUP)], axis=0
    )


def gather_heads(value, lanes, width):
    total = jnp.where(lanes // width == 0, value[:PAD], 0.0)
    for h in range(1, GROUP):
        total = jnp.where(lanes // width == h, value[h * PAD : (h + 1) * PAD], total)
    return total


class Exchange:
    def __init__(self, grad, recvs, send_sem, recv_sem, chunk, where):
        self.grad, self.recvs, self.send_sem, self.recv_sem = grad, recvs, send_sem, recv_sem
        self.chunk, self.where, self.step = chunk, where, 0

    def copy(self, half, step):
        bits, partners = self.where[half]
        src = self.grad.at[(half, *bits[:step], 1 - bits[step])]
        return pltpu.make_async_remote_copy(
            src_ref=src,
            dst_ref=self.recvs[step].at[half],
            send_sem=self.send_sem.at[self.chunk, half, step],
            recv_sem=self.recv_sem.at[self.chunk, half, step],
            device_id=partners[step],
            device_id_type=MESH,
        )

    def start(self):
        for half in range(2):
            self.copy(half, 0).start()

    def advance(self):
        step = self.step
        if step >= STEPS:
            return
        for half in range(2):
            self.copy(half, step).wait()
            bits = self.where[half][0]
            at = (half, *bits[: step + 1])
            self.grad[at] = self.grad[at] + self.recvs[step][half]
            if step + 1 < STEPS:
                self.copy(half, step + 1).start()
        self.step += 1


def kernel(dims, *refs):
    win, count, dim, heads, entries, remote = dims
    width = dim // heads
    groups = heads // GROUP
    scale = width**-0.5
    tok, cot, reg, rel, w_qkv, w_proj, table = refs[:7]
    rest = refs[7:]
    if remote:
        out, out_table = rest[:2]
        rest = rest[2:]
    else:
        out_qkv, out_proj, out_table = rest[:3]
        rest = rest[3:]
    x, xt, c, qkv, d_att, att, d_qkv, probs, masks, bias, bias_rows, d_bias, small, rel_t, tab = rest[:15]
    rest = rest[15:]
    if remote:
        tab_buf, tab_recv, tab_send, tab_sem, send_sem, recv_sem, grad_p, grad_q = rest[:8]
        recv_p, recv_q = rest[8 : 8 + STEPS], rest[8 + STEPS : 8 + 2 * STEPS]
        gx, gy, gz = (lax.axis_index(a) for a in AXES)
        core, ypos, z0, z1 = gz % 2, gz // 2, gy % 2, gy // 2
        to_core = (gx, gy, gz + 1 - 2 * core)
        to_x = (1 - gx, gy, gz)
        to_y = (gx, gy, gz + 2 - 4 * ypos)
        to_z0 = (gx, gy + 1 - 2 * z0, gz)
        to_z1 = (gx, gy + 2 - 4 * z1, gz)
        where = (
            ((core, gx, ypos, z0, z1), (to_core, to_x, to_y, to_z0, to_z1)),
            ((core, ypos, gx, z0, z1), (to_core, to_y, to_x, to_z0, to_z1)),
        )
        barrier = pltpu.get_barrier_semaphore()
        for there in where[0][1]:
            pl.semaphore_signal(barrier, inc=1, device_id=there, device_id_type=MESH)
        pl.semaphore_wait(barrier, STEPS)

    lanes = lax.broadcasted_iota(jnp.int32, (PAD, GROUP * width), 1)

    x[...] = jnp.zeros_like(x)
    c[...] = jnp.zeros_like(c)
    for w in range(win):
        x[pl.ds(w * PAD, count), :] = tok[w]
        c[pl.ds(w * PAD, count), :] = cot[w]
    rows_all = win * PAD

    @pl.loop(0, rows_all // 256)
    def _(i):
        rows = pl.ds(pl.multiple_of(i * 256, 256), 256)
        qkv[rows, :] = dot(x[rows, :], w_qkv[...]).astype(BF16)
        d_att[rows, :] = dot(c[rows, :], w_proj[...], NT).astype(BF16)

    xt[...] = x[...].T

    small[...] = jnp.zeros_like(small)
    small[0:win, 0:count] = reg[...].astype(F32)
    reg_rows = small[...]
    reg_cols = reg_rows.T
    for w in range(win):
        row = reg_rows[w : w + 1, :PAD]
        row = jnp.concatenate([row, row], axis=1)
        masks[w * PAD : (w + 1) * PAD, :] = jnp.where(
            reg_cols[:PAD, w : w + 1] == row, 0.0, -100.0 * LOG2E
        )

    small[...] = jnp.full_like(small, -1.0)
    small[0:count, 0:count] = rel[...].astype(F32)
    rel_t[...] = small[...].T
    tab[...] = jnp.zeros_like(tab)
    tab[0:entries, 0:heads] = table[...]
    size = tab.shape[0]
    tab_t = tab[...].T[:heads]
    high = tab_t.astype(BF16)
    low = (tab_t - high.astype(F32)).astype(BF16)
    both = jnp.concatenate([high, low], axis=0)
    entry = lax.broadcasted_iota(jnp.int32, (size, 128), 0).astype(F32)

    def one_hot(j):
        return jnp.where(entry == rel_t[pl.ds(j, 1), :], 1.0, 0.0).astype(BF16)

    bias_rows[...] = jnp.full_like(bias_rows, -1e30)

    def look(j, carry):
        found = dot(both, one_hot(j))
        bias_rows[pl.ds(pl.multiple_of(j * heads, heads), heads), :] = (
            found[:heads] + found[heads:]
        ) * LOG2E
        return carry

    lax.fori_loop(0, count, look, 0)
    for g in range(groups):
        bias[g] = jnp.concatenate(
            [bias_rows[pl.ds(g * GROUP + h, PAD, stride=heads), :][:, :PAD] for h in range(GROUP)],
            axis=1,
        )
    d_bias[...] = jnp.zeros_like(d_bias)

    def rows_of(w):
        return pl.ds(pl.multiple_of(w * PAD, PAD), PAD)

    def part(ref, which, g, rows):
        at = which * dim + g * GROUP * width
        return ref[rows, at : at + GROUP * width]

    def forward(w, carry):
        rows = rows_of(w)
        mask = masks[rows, :]
        mask = jnp.concatenate([mask] * (GROUP * PAD // 128), axis=1)
        for g in range(groups):
            queries = spread(part(qkv, 0, g, rows), lanes, width)
            scores = dot(part(qkv, 1, g, rows), queries, NT)
            scores = scores * (scale * LOG2E) + bias[g] + mask
            raised = jnp.exp2(scores - jnp.max(scores, axis=0, keepdims=True))
            p = (raised * (1.0 / jnp.sum(raised, axis=0, keepdims=True))).astype(BF16)
            probs[g, rows, :] = p
            mixed = dot(p, part(qkv, 2, g, rows), TN)
            at = g * GROUP * width
            att[rows, at : at + GROUP * width] = gather_heads(mixed, lanes, width).astype(BF16)
        return carry

    lax.fori_loop(0, win, forward, 0)

    def place(value, ref):
        for d in range(value.shape[0] // 16):
            dx, dy, dz = d // 16, (d // 4) % 4, d % 4
            for half in range(2):
                a, b = (dx, dz // 2) if half == 0 else (dz // 2, dx)
                block = value[16 * d + 8 * half : 16 * d + 8 * half + 8]
                ref[half, dz % 2, a, b, dy % 2, dy // 2] = block

    g_proj = dot(att[...], c[...], TN)
    active = []
    if remote:
        place(g_proj, grad_p)
        active.append(Exchange(grad_p, recv_p, send_sem, recv_sem, 0, where))
        active[0].start()
    else:
        out_proj[...] = g_proj

    def backward(g):
        def one(w, carry):
            rows = rows_of(w)
            queries = spread(part(qkv, 0, g, rows), lanes, width)
            d_out = spread(part(d_att, 0, g, rows), lanes, width)
            p = probs[g, rows, :]
            d_probs = dot(part(qkv, 2, g, rows), d_out, NT)
            pf = p.astype(F32)
            weighted = pf * d_probs
            d_scores = weighted - pf * jnp.sum(weighted, axis=0, keepdims=True)
            d_bias[g] += d_scores
            ds = d_scores.astype(BF16)
            d_v = dot(p, d_out)
            d_k = dot(ds, queries) * scale
            d_q = gather_heads(dot(ds, part(qkv, 1, g, rows), TN), lanes, width) * scale
            d_qkv[rows, :] = jnp.concatenate([d_q, d_k, d_v], axis=1).astype(BF16)
            return carry

        return one

    pieces = 4
    wide = GROUP * width
    for g in range(groups):
        for s in range(pieces):
            lax.fori_loop(s * win // pieces, (s + 1) * win // pieces, backward(g), 0, unroll=2)
            for each in active:
                each.advance()
        g_qkv = dot(xt[...], d_qkv[...])
        if remote:
            place(g_qkv, grad_q.at[g])
            active.append(Exchange(grad_q.at[g], [r.at[g] for r in recv_q], send_sem, recv_sem, g + 1, where))
            active[-1].start()
        else:
            for which in range(3):
                at = which * dim + g * wide
                out_qkv[:, at : at + wide] = g_qkv[:, which * wide : (which + 1) * wide]

    for each in active:
        each.advance()

    for g in range(groups):
        for h in range(GROUP):
            piece = d_bias[g, :, h * PAD : (h + 1) * PAD]
            bias_rows[pl.ds(g * GROUP + h, PAD, stride=heads), :] = jnp.concatenate(
                [piece, jnp.zeros_like(piece)], axis=1
            )

    def collect(j, total):
        value = bias_rows[pl.ds(pl.multiple_of(j * heads, heads), heads), :]
        top = value.astype(BF16)
        rest_of = (value - top.astype(F32)).astype(BF16)
        return total + dot(jnp.concatenate([top, rest_of], axis=0), one_hot(j), NT)

    g_table = lax.fori_loop(0, count, collect, jnp.zeros((2 * heads, size), F32))
    g_table = g_table[:heads] + g_table[heads:]
    if not remote:
        out_table[...] = g_table
        return

    tab_buf[0] = g_table
    for step in range(STEPS):
        sent = pltpu.make_async_remote_copy(
            src_ref=tab_buf.at[step],
            dst_ref=tab_recv.at[step],
            send_sem=tab_send.at[step],
            recv_sem=tab_sem.at[step],
            device_id=where[0][1][step],
            device_id_type=MESH,
        )
        sent.start()
        for each in active:
            each.advance()
        sent.wait()
        tab_buf[step + 1] = tab_buf[step] + tab_recv[step]
    for each in active:
        while each.step < STEPS:
            each.advance()
    out_table[...] = tab_buf[STEPS]
    for half in range(2):
        bits = where[half][0]
        rows = pl.ds(8 * half, 8)
        out[rows, 3 * dim :] = grad_p[(half, *bits)]
        for g in range(groups):
            done = grad_q[(g, half, *bits)]
            for which in range(3):
                at = which * dim + g * wide
                out[rows, at : at + wide] = done[:, which * wide : (which + 1) * wide]


def local_grads(remote, tokens, cotangent, regions, rel_index, w_qkv, w_proj, bias_table):
    win, count, dim = tokens.shape
    entries, heads = bias_table.shape
    groups = heads // GROUP
    rows = win * PAD
    wide = GROUP * (dim // heads)
    size = -(-entries // 128) * 128
    scratch = [
        pltpu.VMEM((rows, dim), BF16),
        pltpu.VMEM((dim, rows), BF16),
        pltpu.VMEM((rows, dim), BF16),
        pltpu.VMEM((rows, 3 * dim), BF16),
        pltpu.VMEM((rows, dim), BF16),
        pltpu.VMEM((rows, dim), BF16),
        pltpu.VMEM((rows, 3 * wide), BF16),
        pltpu.VMEM((groups, rows, GROUP * PAD), BF16),
        pltpu.VMEM((rows, 128), F32),
        pltpu.VMEM((groups, PAD, GROUP * PAD), F32),
        pltpu.VMEM((PAD * heads, 128), F32),
        pltpu.VMEM((groups, PAD, GROUP * PAD), F32),
        pltpu.VMEM((128, 128), F32),
        pltpu.VMEM((128, 128), F32),
        pltpu.VMEM((size, 128), F32),
    ]
    if remote:
        outs = ((dim // lax.axis_size(AXES), 4 * dim), (heads, size))
        scratch += [
            pltpu.VMEM((STEPS + 1, heads, size), F32),
            pltpu.VMEM((STEPS, heads, size), F32),
            pltpu.SemaphoreType.DMA((STEPS,)),
            pltpu.SemaphoreType.DMA((STEPS,)),
            pltpu.SemaphoreType.DMA((groups + 1, 2, STEPS)),
            pltpu.SemaphoreType.DMA((groups + 1, 2, STEPS)),
            pltpu.VMEM((2,) + (2,) * STEPS + (8, dim), F32),
            pltpu.VMEM((groups, 2) + (2,) * STEPS + (8, 3 * wide), F32),
        ]
        for step in range(STEPS):
            scratch.append(pltpu.VMEM((2,) + (2,) * (STEPS - 1 - step) + (8, dim), F32))
        for step in range(STEPS):
            scratch.append(
                pltpu.VMEM((groups, 2) + (2,) * (STEPS - 1 - step) + (8, 3 * wide), F32)
            )
        params = dict(collective_id=0, has_side_effects=True)
    else:
        outs = ((dim, 3 * dim), (dim, dim), (heads, size))
        params = dict()
    dims = (win, count, dim, heads, entries, remote)
    vmem = pl.BlockSpec(memory_space=pltpu.VMEM)
    return pl.pallas_call(
        functools.partial(kernel, dims),
        out_shape=[jax.ShapeDtypeStruct(o, F32) for o in outs],
        in_specs=[vmem] * 7,
        out_specs=[vmem] * len(outs),
        scratch_shapes=scratch,
        compiler_params=pltpu.CompilerParams(vmem_limit_bytes=60 * 1024 * 1024, **params),
    )(tokens, cotangent, regions, rel_index, w_qkv, w_proj, bias_table)


def body(
    tokens, cotangent, regions, rel_index, w_qkv, w_proj, bias_table, mom_qkv, mom_proj, mom_table
):
    dim = tokens.shape[2]
    entries = bias_table.shape[0]
    devices = lax.axis_size(AXES)
    sizes = tuple(lax.axis_size(a) for a in AXES)
    scale = 1.0 / (tokens.shape[0] * devices)
    args = (tokens, cotangent, regions, rel_index, w_qkv, w_proj, bias_table)
    if sizes == (2, 4, 4) and dim == 16 * devices:
        mine, table = local_grads(True, *args)
        qkv_mine, proj_mine = mine[:, : 3 * dim].reshape(-1), mine[:, 3 * dim :].reshape(-1)
    else:
        qkv, proj, table = local_grads(False, *args)
        qkv_mine = lax.psum_scatter(qkv.reshape(-1), AXES, tiled=True)
        proj_mine = lax.psum_scatter(proj.reshape(-1), AXES, tiled=True)
        table = lax.psum(table, AXES)
    return (
        0.9 * mom_qkv + qkv_mine * scale,
        0.9 * mom_proj + proj_mine * scale,
        0.9 * mom_table + table[:, :entries].T * scale,
    )


def solution(mesh):
    return jax.shard_map(
        body,
        mesh=mesh,
        in_specs=(
            P(AXES, None, None),
            P(AXES, None, None),
            P(AXES, None),
            P(),
            P(),
            P(),
            P(),
            P(AXES),
            P(AXES),
            P(),
        ),
        out_specs=(P(AXES), P(AXES), P()),
        check_vma=False,
    )
```

profile of v0, /device:TPU:0, one launch (start us, length us, event | category | flops | bytes accessed | tf_op | source)
XLA Modules:
  0.0 118.7 jit_solution(1787983521793130170)
XLA Ops:
  0.6 0.0 copy-start
  0.6 1.5 %copy.15.refs_6_ = f32[169,16]{1,0:T(8,128)} copy(f32[169,16]{0,1:T(8,128)} %param.16) | data formatting | bytes 21632 | tf_op args[6]
  2.2 2.5 %copy.13.refs_0_ = bf16[16,49,512]{2,1,0:T(8,128)(2,1)} copy(bf16[16,49,512]{2,0,1:T(8,128)(2,1)} %param.10) | data formatting | bytes 1605632 | tf_op args[0]
  4.7 0.0 copy-done
  4.7 1.4 %copy.14.refs_1_ = bf16[16,49,512]{2,1,0:T(8,128)(2,1)} copy(bf16[16,49,512]{2,0,1:T(8,128)(2,1)S(1)} %copy-done) | data formatting | bytes 1605632 | tf_op args[1]
  6.1 0.0 copy-start.3
  6.1 0.0 copy-start.1
  6.1 0.0 copy-start.2
  6.1 108.3 %shard_map.121 = (f32[16,2048]{1,0:T(8,128)}, f32[16,256]{1,0:T(8,128)}) custom-call(bf16[16,49,512]{2,1,0:T(8,128)(2,1)} %copy.13.refs_0_, bf16[16,49,512]{2,1,0:T(8,128)(2,1)} %copy.14.refs_1_, s32[16,49]{1,0:T(8,128)} %refs_2_.1, s32[49,49]{1,0:T(8,128)} %refs_3_.1, bf16[512,1536]{1,0:T(8,128)(2,1)} %refs_4_.1, bf16[512,512]{1,0:T(8,128)(2,1)} %refs_5_.1, ...), custom_call_target="tpu_custom_call" | custom-call | tf_op jit(solution)/shard_map/pallas_call | solution.py:347
  114.4 0.0 copy-done.3
  114.4 1.3 %bitcast_add_fusion = f32[169,16]{0,1:T(8,128)} fusion(f32[16,256]{1,0:T(8,128)} %get-tuple-element.6, f32[169,16]{0,1:T(8,128)S(1)} %copy-done.3), kind=kLoop, calls=%fused_computation.4 | loop fusion | flops 8112 | bytes 32448 | tf_op jit(solution)/shard_map/add | solution.py:377
  115.7 0.8 multiply_bitcast_fusion
  116.5 0.9 slice_multiply_fusion
  117.4 0.0 copy-done.1
  117.4 0.7 multiply_add_fusion
  118.1 0.0 copy-done.2
  118.1 0.6 multiply_add_fusion.1
  (2 shorter events, 0.0 us)
Async XLA Ops:
  0.6 4.1 %copy-start = (bf16[16,49,512]{2,0,1:T(8,128)(2,1)S(1)}, bf16[16,49,512]{2,0,1:T(8,128)(2,1)}, u32[]{:S(2)}) copy-start(bf16[16,49,512]{2,0,1:T(8,128)(2,1)} %param.11) | copy-start | bytes 2408452
  6.1 108.3 %copy-start.3 = (f32[169,16]{0,1:T(8,128)S(1)}, f32[169,16]{0,1:T(8,128)}, u32[]{:S(2)}) copy-start(f32[169,16]{0,1:T(8,128)} %param.19) | copy-start | bytes 32452
  6.1 111.3 %copy-start.1 = (f32[24576]{0:T(1024)S(1)}, f32[24576]{0:T(1024)}, u32[]{:S(2)}) copy-start(f32[24576]{0:T(1024)} %param.17) | copy-start | bytes 294916
  6.1 112.0 %copy-start.2 = (f32[8192]{0:T(1024)S(1)}, f32[8192]{0:T(1024)}, u32[]{:S(2)}) copy-start(f32[8192]{0:T(1024)} %param.18) | copy-start | bytes 98308
where the time goes:
time: 119 us
  Pallas kernels  108 us (91%)
  local copies, waits for them, and re-layouts  5.48 us (5%)
  other arithmetic  4.27 us (4%)
    pallas_call x1, Pallas kernels, local_grads(): pl.pallas_call(functools.partial(kernel, dims), out_shape=[jax.ShapeDtype...  108 us
    unnamed x12, local copies, waits for them, and re-layouts  5.47 us

commit v1 on v0

--- a/solution.py
+++ b/solution.py
@@ -166,7 +166,8 @@
     d_bias[...] = jnp.zeros_like(d_bias)
 
     def rows_of(w):
-        return pl.ds(pl.multiple_of(w * PAD, PAD), PAD)
+        at = w * PAD
+        return pl.ds(at if isinstance(at, int) else pl.multiple_of(at, PAD), PAD)
 
     def part(ref, which, g, rows):
         at = which * dim + g * GROUP * width
@@ -176,16 +177,17 @@
         rows = rows_of(w)
         mask = masks[rows, :]
         mask = jnp.concatenate([mask] * (GROUP * PAD // 128), axis=1)
-        for g in range(groups):
-            queries = spread(part(qkv, 0, g, rows), lanes, width)
-            scores = dot(part(qkv, 1, g, rows), queries, NT)
-            scores = scores * (scale * LOG2E) + bias[g] + mask
-            raised = jnp.exp2(scores - jnp.max(scores, axis=0, keepdims=True))
-            p = (raised * (1.0 / jnp.sum(raised, axis=0, keepdims=True))).astype(BF16)
-            probs[g, rows, :] = p
-            mixed = dot(p, part(qkv, 2, g, rows), TN)
-            at = g * GROUP * width
-            att[rows, at : at + GROUP * width] = gather_heads(mixed, lanes, width).astype(BF16)
+        every = range(groups)
+        queries = [spread(part(qkv, 0, g, rows), lanes, width) for g in every]
+        scores = [dot(part(qkv, 1, g, rows), queries[g], NT) for g in every]
+        scores = [scores[g] * (scale * LOG2E) + bias[g] + mask for g in every]
+        raised = [jnp.exp2(v - jnp.max(v, axis=0, keepdims=True)) for v in scores]
+        p = [(v * (1.0 / jnp.sum(v, axis=0, keepdims=True))).astype(BF16) for v in raised]
+        mixed = [dot(p[g], part(qkv, 2, g, rows), TN) for g in every]
+        joined = [gather_heads(v, lanes, width).astype(BF16) for v in mixed]
+        att[rows, :] = jnp.concatenate(joined, axis=1)
+        for g in every:
+            probs[g, rows, :] = p[g]
         return carry
 
     lax.fori_loop(0, win, forward, 0)
@@ -207,31 +209,32 @@
     else:
         out_proj[...] = g_proj
 
-    def backward(g):
-        def one(w, carry):
-            rows = rows_of(w)
-            queries = spread(part(qkv, 0, g, rows), lanes, width)
-            d_out = spread(part(d_att, 0, g, rows), lanes, width)
-            p = probs[g, rows, :]
-            d_probs = dot(part(qkv, 2, g, rows), d_out, NT)
-            pf = p.astype(F32)
-            weighted = pf * d_probs
-            d_scores = weighted - pf * jnp.sum(weighted, axis=0, keepdims=True)
-            d_bias[g] += d_scores
-            ds = d_scores.astype(BF16)
-            d_v = dot(p, d_out)
-            d_k = dot(ds, queries) * scale
-            d_q = gather_heads(dot(ds, part(qkv, 1, g, rows), TN), lanes, width) * scale
-            d_qkv[rows, :] = jnp.concatenate([d_q, d_k, d_v], axis=1).astype(BF16)
-            return carry
-
-        return one
+    def backward(g, windows):
+        rows = [rows_of(w) for w in windows]
+        queries = [spread(part(qkv, 0, g, r), lanes, width) for r in rows]
+        d_out = [spread(part(d_att, 0, g, r), lanes, width) for r in rows]
+        p = [probs[g, r, :] for r in rows]
+        every = range(len(rows))
+        d_probs = [dot(part(qkv, 2, g, rows[n]), d_out[n], NT) for n in every]
+        d_v = [dot(p[n], d_out[n]) for n in every]
+        pf = [v.astype(F32) for v in p]
+        weighted = [pf[n] * d_probs[n] for n in every]
+        d_scores = [
+            weighted[n] - pf[n] * jnp.sum(weighted[n], axis=0, keepdims=True) for n in every
+        ]
+        d_bias[g] += sum(d_scores[1:], d_scores[0])
+        ds = [v.astype(BF16) for v in d_scores]
+        d_k = [dot(ds[n], queries[n]) * scale for n in every]
+        d_q = [dot(ds[n], part(qkv, 1, g, rows[n]), TN) for n in every]
+        d_q = [gather_heads(v, lanes, width) * scale for v in d_q]
+        for n in every:
+            d_qkv[rows[n], :] = jnp.concatenate([d_q[n], d_k[n], d_v[n]], axis=1).astype(BF16)
 
     pieces = 4
     wide = GROUP * width
     for g in range(groups):
         for s in range(pieces):
-            lax.fori_loop(s * win // pieces, (s + 1) * win // pieces, backward(g), 0, unroll=2)
+            backward(g, range(s * win // pieces, (s + 1) * win // pieces))
             for each in active:
                 each.advance()
         g_qkv = dot(xt[...], d_qkv[...])

time: 119 us -> 116 us (0.975)
  Pallas kernels: 108 us -> 105 us
    pallas_call x1, Pallas kernels: 108 us -> 105 us  [local_grads(): pl.pallas_call(functools.partial(kernel, dims), out_shape=[jax.ShapeDtype...]
where the time goes in v1:
time: 116 us; the launch traced here: 115 us
  Pallas kernels  105 us (91%)
  local copies, waits for them, and re-layouts  5.48 us (5%)
  other arithmetic  4.27 us (4%)
    pallas_call x1, Pallas kernels, local_grads(): pl.pallas_call(functools.partial(kernel, dims), out_shape=[jax.ShapeDtype...  105 us
    unnamed x12, local copies, waits for them, and re-layouts  5.47 us

profile of v1, /device:TPU:0, one launch (start us, length us, event | category | flops | bytes accessed | tf_op | source)
XLA Modules:
  0.0 115.2 jit_solution(11571482934375317902)
XLA Ops:
  0.6 0.0 copy-start
  0.6 1.5 %copy.15.refs_6_ = f32[169,16]{1,0:T(8,128)} copy(f32[169,16]{0,1:T(8,128)} %param.16) | data formatting | bytes 21632 | tf_op args[6]
  2.2 2.5 %copy.13.refs_0_ = bf16[16,49,512]{2,1,0:T(8,128)(2,1)} copy(bf16[16,49,512]{2,0,1:T(8,128)(2,1)} %param.10) | data formatting | bytes 1605632 | tf_op args[0]
  4.7 0.0 copy-done
  4.7 1.4 %copy.14.refs_1_ = bf16[16,49,512]{2,1,0:T(8,128)(2,1)} copy(bf16[16,49,512]{2,0,1:T(8,128)(2,1)S(1)} %copy-done) | data formatting | bytes 1605632 | tf_op args[1]
  6.1 0.0 copy-start.3
  6.1 0.0 copy-start.1
  6.1 0.0 copy-start.2
  6.1 104.7 %shard_map.121 = (f32[16,2048]{1,0:T(8,128)}, f32[16,256]{1,0:T(8,128)}) custom-call(bf16[16,49,512]{2,1,0:T(8,128)(2,1)} %copy.13.refs_0_, bf16[16,49,512]{2,1,0:T(8,128)(2,1)} %copy.14.refs_1_, s32[16,49]{1,0:T(8,128)} %refs_2_.1, s32[49,49]{1,0:T(8,128)} %refs_3_.1, bf16[512,1536]{1,0:T(8,128)(2,1)} %refs_4_.1, bf16[512,512]{1,0:T(8,128)(2,1)} %refs_5_.1, ...), custom_call_target="tpu_custom_call" | custom-call | tf_op jit(solution)/shard_map/pallas_call | solution.py:350
  110.8 0.0 copy-done.3
  110.8 1.3 %bitcast_add_fusion = f32[169,16]{0,1:T(8,128)} fusion(f32[16,256]{1,0:T(8,128)} %get-tuple-element.6, f32[169,16]{0,1:T(8,128)S(1)} %copy-done.3), kind=kLoop, calls=%fused_computation.4 | loop fusion | flops 8112 | bytes 32448 | tf_op jit(solution)/shard_map/add | solution.py:380
  112.2 0.8 multiply_bitcast_fusion
  112.9 0.9 slice_multiply_fusion
  113.8 0.0 copy-done.1
  113.8 0.7 multiply_add_fusion
  114.5 0.0 copy-done.2
  114.5 0.6 multiply_add_fusion.1
  (2 shorter events, 0.0 us)
Async XLA Ops:
  0.6 4.1 %copy-start = (bf16[16,49,512]{2,0,1:T(8,128)(2,1)S(1)}, bf16[16,49,512]{2,0,1:T(8,128)(2,1)}, u32[]{:S(2)}) copy-start(bf16[16,49,512]{2,0,1:T(8,128)(2,1)} %param.11) | copy-start | bytes 2408452
  6.1 104.7 %copy-start.3 = (f32[169,16]{0,1:T(8,128)S(1)}, f32[169,16]{0,1:T(8,128)}, u32[]{:S(2)}) copy-start(f32[169,16]{0,1:T(8,128)} %param.19) | copy-start | bytes 32452
  6.1 107.8 %copy-start.1 = (f32[24576]{0:T(1024)S(1)}, f32[24576]{0:T(1024)}, u32[]{:S(2)}) copy-start(f32[24576]{0:T(1024)} %param.17) | copy-start | bytes 294916
  6.1 108.4 %copy-start.2 = (f32[8192]{0:T(1024)S(1)}, f32[8192]{0:T(1024)}, u32[]{:S(2)}) copy-start(f32[8192]{0:T(1024)} %param.18) | copy-start | bytes 98308
